TPU v7x, 512 devices: a whole 4x4x16 slice. The times are simulated.
512 devices in a mesh: seq: 64 (over x, z), head: 8 (over y, core).
Axes of the slice: x: 4, y: 4, z: 16, core: 2. Of those that a mesh axis runs over, the one named last changes fastest.
Arguments:
- queries: bfloat16 [16384, 4096], P('seq', 'head'), may hold values from -12 to 12
- key_input: bfloat16 [16384, 4096], P('seq', 'head'), may hold values from -1.796875 to 1.796875
- value_input: bfloat16 [16384, 4096], P('seq', 'head'), may hold values from -32 to 32
- norm_gain: bfloat16 [4096], P('head'), may hold values from 0.099609375 to 1.8984375
- out_weight: bfloat16 [4096, 3072], P('head', 'seq'), may hold values from -0.25 to 0.25
- target: bfloat16 [16384, 3072], P('seq', 'head'), may hold values from -6 to 6
Outputs:
- output: bfloat16 [16384, 3072], P('seq', 'head')
- query_grad: bfloat16 [16384, 4096], P('seq', 'head')
- key_grad: bfloat16 [16384, 4096], P('seq', 'head')
- value_grad: bfloat16 [16384, 4096], P('seq', 'head')
- gain_grads: float32 [64, 4096], P('seq', 'head')
- weight_grads: bfloat16 [64, 4096, 3072], P('seq', 'head')
All inputs are finite; a program needn't handle non-finite values.
Results may differ from a plain program's by a relative error of at most 0.022.
Values may be sent and summed in bfloat16 or wider, within the bound.
No kernel may reach another device: no remote copies, remote signals or barrier semaphores. Data moves between devices by JAX's collectives and lax.ppermute only.
A program may use at most 64 MiB of HBM per device.

v0:
```python
import functools

import jax
import jax.numpy as jnp
from jax import lax
from jax.experimental import pallas as pl
from jax.experimental.pallas import tpu as pltpu
from jax.sharding import Mesh
from jax.sharding import PartitionSpec as P


HEAD_DIM = 128
FEATURES = 4096
SEQ = ("x", "z")
HEAD = ("y", "c")
EPSILON = 1e-06
F32 = jnp.float32
BF16 = jnp.bfloat16
NX, NZ, NY, NC = 4, 16, 4, 2
VMEM_LIMIT = 16 << 20
EXTRA = 8


def dot(a, b, ca, cb):
    return lax.dot_general(a, b, (((ca,), (cb,)), ((), ())), preferred_element_type=F32)


def call(kernel, outs, args, flops=0):
    moved = sum(a.size * a.dtype.itemsize for a in args)
    moved += sum(o.size * o.dtype.itemsize for o in outs)
    return pl.pallas_call(
        kernel,
        out_shape=outs,
        in_specs=[pl.BlockSpec(memory_space=pltpu.VMEM)] * len(args),
        out_specs=[pl.BlockSpec(memory_space=pltpu.VMEM)] * len(outs),
        cost_estimate=pl.CostEstimate(flops=flops, bytes_accessed=moved, transcendentals=0),
        compiler_params=pltpu.CompilerParams(vmem_limit_bytes=VMEM_LIMIT),
    )(*args)


def arr(shape, dtype):
    return jax.ShapeDtypeStruct(shape, dtype)


def head_cols(h):
    return slice(h * HEAD_DIM, (h + 1) * HEAD_DIM)


def keep_mask(count):
    rows = lax.broadcasted_iota(jnp.int32, (count, count), 0)
    cols = lax.broadcasted_iota(jnp.int32, (count, count), 1)
    return rows >= cols


def row_sums(p):
    high = p.astype(BF16)
    low = (p - high.astype(F32)).astype(BF16)
    ones = jnp.ones((EXTRA, p.shape[1]), BF16)
    return dot(ones, high, 1, 1) + dot(ones, low, 1, 1)


def pack_rows(sums):
    high = sums.astype(BF16).astype(F32)
    low = sums - high
    row = lax.broadcasted_iota(jnp.int32, sums.shape, 0)
    return jnp.where(row < EXTRA // 2, high, low).astype(BF16)


def unpack_rows(packed):
    wide = packed.astype(F32)
    return wide[0:1] + wide[EXTRA // 2 : EXTRA // 2 + 1]


def as_columns(row):
    return jnp.broadcast_to(row, (HEAD_DIM, row.shape[1])).T


def state_kernel(a_ref, b_ref, out_ref):
    for h in range(a_ref.shape[1] // HEAD_DIM):
        cols = head_cols(h)
        out_ref[cols, :] = dot(a_ref[:, cols], b_ref[:, cols], 0, 0).astype(BF16)


def local_kernel(q_ref, k_ref, v_ref, out_ref):
    keep = keep_mask(q_ref.shape[0])
    for h in range(q_ref.shape[1] // HEAD_DIM):
        cols = head_cols(h)
        scores = dot(q_ref[:, cols], k_ref[:, cols], 1, 1)
        scores = jnp.where(keep, scores, 0.0).astype(BF16)
        out_ref[:, cols] = dot(scores, v_ref[:, cols], 1, 0)


def totals_kernel(reverse, in_ref, out_ref):
    total = in_ref[0].astype(F32)
    for i in range(1, NZ):
        total = total + in_ref[i].astype(F32)
    x = lax.axis_index("x")
    for k in range(NX):
        sent = (k < x) if reverse else (k > x)
        out_ref[k] = jnp.where(sent, total, 0.0)


def prefix_kernel(reverse, in_ref, offset_ref, out_ref):
    running = offset_ref[0]
    for k in range(1, NX):
        running = running + offset_ref[k]
    order = range(NZ)
    for i in reversed(order) if reverse else order:
        out_ref[i] = running.astype(BF16)
        running = running + in_ref[i].astype(F32)


def halves(refs, c, width):
    w0_ref, w1_ref, w3_ref, wa_ref, wb_ref = refs
    own = pl.ds(pl.multiple_of(c * width, width), width)
    other = pl.ds(pl.multiple_of((1 - c) * width, width), width)
    first, second = wa_ref[...], wb_ref[...]
    return (
        (lambda: w0_ref[own, :], lambda: w0_ref[other, :]),
        (lambda: w1_ref[own, :], lambda: w1_ref[other, :]),
        (lambda: jnp.where(c == 0, first, second), lambda: jnp.where(c == 0, second, first)),
        (lambda: w3_ref[own, :], lambda: w3_ref[other, :]),
    )


def project_kernel(
    att_ref, q_ref, state_ref, gain_ref, w0_ref, w1_ref, w3_ref, wa_ref, wb_ref,
    mixed_ref, scaled_ref, send_ref, sums_ref,
):
    for h in range(q_ref.shape[1] // HEAD_DIM):
        cols = head_cols(h)
        mixed_ref[:, cols] = att_ref[:, cols] + dot(q_ref[:, cols], state_ref[cols, :], 1, 0)
    mixed = mixed_ref[...]
    scaled = (mixed * gain_ref[...].astype(F32)).astype(BF16)
    scaled_ref[...] = scaled
    sums = row_sums(mixed * mixed)
    sums_ref[...] = sums
    packed = pack_rows(sums)
    x, c = lax.axis_index("x"), lax.axis_index("c")
    count, width = mixed.shape[0], send_ref.shape[2]
    for r, (_, theirs) in enumerate(halves((w0_ref, w1_ref, w3_ref, wa_ref, wb_ref), c, width)):
        place = lax.rem(x + r, NX)
        send_ref[place, 0:count, :] = dot(scaled, theirs(), 1, 1).astype(BF16)
        send_ref[r, count : count + EXTRA, 0:count] = packed
        send_ref[r, count : count + EXTRA, count:width] = jnp.zeros((EXTRA, width - count), BF16)


def project_own_kernel(scaled_ref, w0_ref, w1_ref, w3_ref, wa_ref, wb_ref, keep_ref):
    x, c = lax.axis_index("x"), lax.axis_index("c")
    width = keep_ref.shape[2]
    scaled = scaled_ref[...]
    for r, (mine, _) in enumerate(halves((w0_ref, w1_ref, w3_ref, wa_ref, wb_ref), c, width)):
        keep_ref[lax.rem(x + r, NX)] = dot(scaled, mine(), 1, 1)


def pair_kernel(keep_ref, got_ref, sums_ref, out_ref):
    count, width = keep_ref.shape[1], keep_ref.shape[2]
    sums = sums_ref[...] + unpack_rows(got_ref[0, count : count + EXTRA, 0:count])
    packed = pack_rows(sums)
    for k in range(NY):
        out_ref[k, 0:count, :] = (keep_ref[k] + got_ref[k, 0:count, :].astype(F32)).astype(BF16)
        out_ref[k, count : count + EXTRA, 0:count] = packed
        out_ref[k, count : count + EXTRA, count:width] = jnp.zeros((EXTRA, width - count), BF16)


def output_kernel(got_ref, target_ref, out_ref, grad_ref, inverse_ref):
    count, width = target_ref.shape
    total = got_ref[0, 0:count, :].astype(F32)
    squares = unpack_rows(got_ref[0, count : count + EXTRA, 0:count])
    for k in range(1, NY):
        total = total + got_ref[k, 0:count, :].astype(F32)
        squares = squares + unpack_rows(got_ref[k, count : count + EXTRA, 0:count])
    inverse = lax.rsqrt(squares / FEATURES + EPSILON)
    inverse_ref[...] = jnp.broadcast_to(inverse, inverse_ref.shape)
    scale = as_columns(inverse)
    projected = total * jnp.concatenate([scale] * (width // HEAD_DIM), axis=1)
    out_ref[...] = projected.astype(BF16)
    grad = (projected - target_ref[...].astype(F32)).astype(BF16)
    grad_ref[0:count, :] = grad
    packed = pack_rows(row_sums(grad.astype(F32) * projected))
    grad_ref[count : count + EXTRA, 0:count] = packed
    grad_ref[count : count + EXTRA, count:width] = jnp.zeros((EXTRA, width - count), BF16)


def normed_grad_kernel(
    core, grad_ref, w0_ref, w1_ref, w3_ref, wa_ref, wb_ref, out_ref, inner_ref
):
    count, width = out_ref.shape[0], grad_ref.shape[2]
    x, c = lax.axis_index("x"), lax.axis_index("c")
    total = None
    for r, pair in enumerate(halves((w0_ref, w1_ref, w3_ref, wa_ref, wb_ref), c, width)):
        part = dot(grad_ref[lax.rem(x + r, NX), 0:count, :], pair[core](), 1, 0)
        total = part if total is None else total + part
    out_ref[...] = total
    inner = unpack_rows(grad_ref[0, count : count + EXTRA, 0:count])
    for k in range(1, NY):
        inner = inner + unpack_rows(grad_ref[k, count : count + EXTRA, 0:count])
    inner_ref[...] = jnp.broadcast_to(inner, inner_ref.shape)


def mixed_grad_kernel(
    part_ref, part_inner_ref, other_ref, w0_ref, w1_ref, w3_ref, wa_ref, wb_ref,
    mixed_ref, gain_ref, inverse_ref, q_ref, grad_ref, gain_grad_ref, state_ref,
):
    count = mixed_ref.shape[0]
    width = other_ref.shape[2]
    x, c = lax.axis_index("x"), lax.axis_index("c")
    total = part_ref[...]
    for r, (_, theirs) in enumerate(halves((w0_ref, w1_ref, w3_ref, wa_ref, wb_ref), c, width)):
        total = total + dot(other_ref[lax.rem(x + r, NX), 0:count, :], theirs(), 1, 0)
    inner = part_inner_ref[0:1, :]
    for k in range(NY):
        inner = inner + unpack_rows(other_ref[k, count : count + EXTRA, 0:count])
    inverse = inverse_ref[0:1, :]
    slope = inverse * inverse * inner / FEATURES
    heads = mixed_ref.shape[1] // HEAD_DIM
    scale = jnp.concatenate([as_columns(inverse)] * heads, axis=1)
    slope = jnp.concatenate([as_columns(slope)] * heads, axis=1)
    mixed = mixed_ref[...]
    scaled = scale * total
    grad = (gain_ref[...].astype(F32) * scaled - mixed * slope).astype(BF16)
    grad_ref[...] = grad
    gain_grad_ref[...] = jnp.sum(scaled * mixed, axis=0, keepdims=True)
    for h in range(heads):
        cols = head_cols(h)
        state_ref[cols, :] = dot(q_ref[:, cols], grad[:, cols], 0, 0).astype(BF16)


def weight_grad_kernel(own_ref, other_ref, mixed_ref, gain_ref, inverse_ref, out_ref):
    count = mixed_ref.shape[0]
    width = own_ref.shape[2]
    heads = mixed_ref.shape[1] // HEAD_DIM
    scale = jnp.concatenate([as_columns(inverse_ref[0:1, :])] * heads, axis=1)
    normed = (mixed_ref[...] * scale * gain_ref[...].astype(F32)).astype(BF16)
    turned = normed.T
    c = lax.axis_index("c")
    for k in range(NY):
        for ref, half in ((own_ref, c), (other_ref, 1 - c)):
            start = pl.multiple_of(k * NC * width + half * width, HEAD_DIM)
            out_ref[0, :, pl.ds(start, width)] = dot(turned, ref[k, 0:count, :], 1, 0).astype(BF16)


def local_grad_kernel(
    q_ref, k_ref, v_ref, grad_ref, state_ref, scores_ref, query_ref, key_ref, value_ref
):
    keep = keep_mask(q_ref.shape[0])
    for h in range(q_ref.shape[1] // HEAD_DIM):
        cols = head_cols(h)
        q, k, v, grad = q_ref[:, cols], k_ref[:, cols], v_ref[:, cols], grad_ref[:, cols]
        scores = scores_ref[h]
        pairs = jnp.where(keep, dot(grad, v, 1, 1), 0.0).astype(BF16)
        query = dot(pairs, k, 1, 0) + dot(grad, state_ref[cols, :], 1, 1)
        query_ref[:, cols] = query.astype(BF16)
        key_ref[:, cols] = dot(pairs, q, 0, 0)
        value_ref[:, cols] = dot(scores, grad, 0, 0)


def later_kernel(k_ref, v_ref, key_part_ref, value_part_ref, later_ref, key_ref, value_ref):
    for h in range(k_ref.shape[1] // HEAD_DIM):
        cols = head_cols(h)
        later = later_ref[cols, :]
        key_ref[:, cols] = (key_part_ref[:, cols] + dot(v_ref[:, cols], later, 1, 1)).astype(BF16)
        value = value_part_ref[:, cols] + dot(k_ref[:, cols], later, 1, 0)
        value_ref[:, cols] = value.astype(BF16)


def scores_kernel(q_ref, k_ref, out_ref):
    keep = keep_mask(q_ref.shape[0])
    for h in range(q_ref.shape[1] // HEAD_DIM):
        cols = head_cols(h)
        scores = dot(q_ref[:, cols], k_ref[:, cols], 1, 1)
        out_ref[h] = jnp.where(keep, scores, 0.0).astype(BF16)


def exchanged(blocks, axis):
    return lax.all_to_all(blocks, axis, 0, 0, tiled=True)


def carried(state, reverse):
    rows, cols = state.shape
    blocks = state.reshape(NZ, rows // NZ, cols)
    got = exchanged(blocks, "z")
    (totals,) = call(
        functools.partial(totals_kernel, reverse),
        [arr((NX, rows // NZ, cols), F32)], [got],
    )
    offsets = exchanged(totals, "x")
    (sums,) = call(
        functools.partial(prefix_kernel, reverse),
        [arr(blocks.shape, BF16)], [got, offsets],
    )
    return exchanged(sums, "z").reshape(rows, cols)


def ring(count, step):
    return [(i, (i + step) % count) for i in range(count)]


def work(queries, key_input, value_input, norm_gain, out_weight, target):
    count, feats = queries.shape
    width = target.shape[1]
    swap = [(0, 1), (1, 0)]
    gain = norm_gain.reshape(1, feats)
    mm = 2 * count * feats

    (state_local,) = call(
        state_kernel, [arr((feats, HEAD_DIM), BF16)], [key_input, value_input],
        mm * HEAD_DIM,
    )
    w0 = lax.all_gather(out_weight.T, "z", axis=0, tiled=True)
    w3 = lax.ppermute(w0, "x", ring(NX, 1))
    w1 = lax.ppermute(w0, "x", ring(NX, -1))
    wa = lax.ppermute(w3[:width], "x", ring(NX, 1))
    wb = lax.ppermute(w1[width:], "x", ring(NX, -1))
    weights = [w0, w1, w3, wa, wb]

    (attended,) = call(
        local_kernel, [arr((count, feats), F32)], [queries, key_input, value_input],
        2 * mm * count,
    )
    state_low = carried(state_local, False)
    message = (NY, count + EXTRA, width)
    columns = NY * NC * width
    mixed, scaled, sent, sums = call(
        project_kernel,
        [
            arr((count, feats), F32),
            arr((count, feats), BF16),
            arr(message, BF16),
            arr((EXTRA, count), F32),
        ],
        [attended, queries, state_low, gain, *weights],
        mm * (HEAD_DIM + columns // 2),
    )
    (kept,) = call(
        project_own_kernel, [arr((NY, count, width), F32)], [scaled, *weights],
        mm * columns // 2,
    )
    got = lax.ppermute(sent, "c", swap)
    (paired,) = call(pair_kernel, [arr(message, BF16)], [kept, got, sums])
    arrived = exchanged(paired, "y")
    (scores,) = call(
        scores_kernel, [arr((feats // HEAD_DIM, count, count), BF16)], [queries, key_input],
        mm * count,
    )
    output, grad_local, inverse = call(
        output_kernel,
        [
            arr((count, width), BF16),
            arr((count + EXTRA, width), BF16),
            arr((EXTRA, count), F32),
        ],
        [arrived, target],
    )
    own = lax.all_gather(grad_local, "y", axis=0, tiled=True).reshape(message)
    other = lax.ppermute(own, "c", swap)
    part, part_inner = call(
        functools.partial(normed_grad_kernel, 0),
        [arr((count, feats), F32), arr((EXTRA, count), F32)], [own, *weights],
        mm * columns // 2,
    )
    mixed_grad, gain_grads, grad_state = call(
        mixed_grad_kernel,
        [arr((count, feats), BF16), arr((1, feats), F32), arr((feats, HEAD_DIM), BF16)],
        [part, part_inner, other, *weights, mixed, gain, inverse, queries],
        mm * (HEAD_DIM + columns // 2),
    )
    (weight_grads,) = call(
        weight_grad_kernel, [arr((1, feats, columns), BF16)],
        [own, other, mixed, gain, inverse], mm * columns,
    )
    query_grad, key_part, value_part = call(
        local_grad_kernel,
        [arr((count, feats), BF16), arr((count, feats), F32), arr((count, feats), F32)],
        [queries, key_input, value_input, mixed_grad, state_low, scores],
        mm * (4 * count + HEAD_DIM),
    )
    later_low = carried(grad_state, True)
    key_grad, value_grad = call(
        later_kernel, [arr((count, feats), BF16)] * 2,
        [key_input, value_input, key_part, value_part, later_low], 2 * mm * HEAD_DIM,
    )
    return output, query_grad, key_grad, value_grad, gain_grads, weight_grads


def solution(mesh):
    torus = Mesh(mesh.devices.reshape(NX, NZ, NY, NC), ("x", "z", "y", "c"))
    return jax.shard_map(
        work,
        mesh=torus,
        in_specs=(
            P(SEQ, HEAD),
            P(SEQ, HEAD),
            P(SEQ, HEAD),
            P(HEAD),
            P(HEAD, SEQ),
            P(SEQ, HEAD),
        ),
        out_specs=(
            P(SEQ, HEAD),
            P(SEQ, HEAD),
            P(SEQ, HEAD),
            P(SEQ, HEAD),
            P(SEQ, HEAD),
            P(SEQ, HEAD, None),
        ),
        check_vma=False,
    )
```

profile of v0, /device:TPU:24, one launch (start us, length us, event | category | flops | bytes accessed | tf_op | source)
XLA Modules:
  0.0 199.9 jit_solution(11997828899725416668)
XLA Ops:
  0.7 40.5 %all_gather.6.w0_ref = bf16[768,512]{1,0:T(8,128)(2,1)S(1)} all-gather(bf16[48,512]{1,0:T(8,128)(2,1)} %bitcast.14), channel_id=1, replica_groups=mesh['x'=4,'z'=16,'y'=4,'c'=2] {'z'}, dimensions={0}, use_global_device_ids=true | all-gather | bytes 835584 | tf_op jit(solution)/shard_map/all_gather | solution.py:310
  41.2 3.4 %collective-permute-start.1 = (bf16[768,512]{1,0:T(8,128)(2,1)S(1)}, bf16[768,512]{1,0:T(8,128)(2,1)S(1)}, u32[]{:S(2)}, u32[]{:S(2)}) collective-permute-start(bf16[768,512]{1,0:T(8,128)(2,1)S(1)} %all_gather.6.w0_ref), channel_id=1, source_target_pairs={{0,128},{128,256},{256,384},{384,0},{1,129},{129,257},{257,385},{3... | collective-permute-start | bytes 2359304 | tf_op jit(solution)/shard_map/ppermute | solution.py:311
  44.6 3.7 %collective-permute-start = (bf16[768,512]{1,0:T(8,128)(2,1)S(1)}, bf16[768,512]{1,0:T(8,128)(2,1)S(1)}, u32[]{:S(2)}, u32[]{:S(2)}) collective-permute-start(bf16[768,512]{1,0:T(8,128)(2,1)S(1)} %all_gather.6.w0_ref), channel_id=1, source_target_pairs={{0,384},{128,0},{256,128},{384,256},{1,385},{129,1},{257,129},{385... | collective-permute-start | bytes 2359304 | tf_op jit(solution)/shard_map/ppermute | solution.py:312
  48.3 0.9 copy-done.1
  49.2 0.9 copy-done.7
  50.4 19.5 %all_to_all.35.in_ref = bf16[16,32,128]{2,1,0:T(8,128)(2,1)S(1)} all-to-all(bf16[16,32,128]{2,1,0:T(8,128)(2,1)S(1)} %bitcast.11), channel_id=1, replica_groups=mesh['x'=4,'z'=16,'y'=4,'c'=2] {'z'}, dimensions={0} | all-to-all | bytes 262144 | tf_op jit(solution)/shard_map/all_to_all | solution.py:276
  70.0 8.5 %all_to_all.36.offset_ref = f32[4,32,128]{2,1,0:T(8,128)S(1)} all-to-all(f32[4,32,128]{2,1,0:T(8,128)S(1)} %shard_map.111), channel_id=1, replica_groups=mesh['x'=4,'z'=16,'y'=4,'c'=2] {'x'}, dimensions={0} | all-to-all | bytes 131072 | tf_op jit(solution)/shard_map/all_to_all | solution.py:276
  79.1 4.0 %all-to-all-start.2 = ((bf16[16,32,128]{2,1,0:T(8,128)(2,1)}), bf16[16,32,128]{2,1,0:T(8,128)(2,1)S(1)}, u32[]{:S(2)}, u32[]{:S(2)}) async-start(bf16[16,32,128]{2,1,0:T(8,128)(2,1)} %shard_map.112), calls=%async_computation.2 | async-start | bytes 262144 | tf_op jit(solution)/shard_map/all_to_all | solution.py:276
  84.0 2.5 %collective-permute-start.2 = (bf16[384,512]{1,0:T(8,128)(2,1)}, bf16[384,512]{1,0:T(8,128)(2,1)S(1)}, u32[]{:S(2)}, u32[]{:S(2)}) collective-permute-start(bf16[384,512]{1,0:T(8,128)(2,1)} %slice.8), channel_id=1, source_target_pairs={{0,128},{128,256},{256,384},{384,0},{1,129},{129,257},{257,385},{3... | collective-permute-start | bytes 1179656 | tf_op jit(solution)/shard_map/ppermute | solution.py:313
  87.2 4.6 %collective-permute-start.3 = (bf16[384,512]{1,0:T(8,128)(2,1)}, bf16[384,512]{1,0:T(8,128)(2,1)}, u32[]{:S(2)}, u32[]{:S(2)}) collective-permute-start(bf16[384,512]{1,0:T(8,128)(2,1)} %slice.9), channel_id=1, source_target_pairs={{0,384},{128,0},{256,128},{384,256},{1,385},{129,1},{257,129},{385... | collective-permute-start | bytes 1179656 | tf_op jit(solution)/shard_map/ppermute | solution.py:314
  94.2 2.0 %all-to-all-done.2 = bf16[16,32,128]{2,1,0:T(8,128)(2,1)S(1)} async-done(((bf16[16,32,128]{2,1,0:T(8,128)(2,1)}), bf16[16,32,128]{2,1,0:T(8,128)(2,1)S(1)}, u32[]{:S(2)}, u32[]{:S(2)}) %all-to-all-start.2) | async-done | bytes 131104 | tf_op jit(solution)/shard_map/all_to_all | solution.py:276
  96.3 1.1 collective-permute-done.3.wb_ref
  97.4 1.0 copy-done.16
  98.4 2.0 %shard_map.113 = (f32[256,512]{1,0:T(8,128)S(1)}, bf16[256,512]{1,0:T(8,128)(2,1)S(1)}, bf16[4,264,384]{2,1,0:T(8,128)(2,1)S(1)}, f32[8,256]{1,0:T(8,128)S(1)}) custom-call(f32[256,512]{1,0:T(8,128)S(1)} %copy-done.16, bf16[256,512]{1,0:T(8,128)(2,1)S(1)} %copy-done, bf16[512,128]{1,0:T(8,128)(2,1)S(1)} %bitcast.9, bf16[1,512]{1,0:T(2,128)(2,1)S(1)} %reshape.32.gain_ref, ...), custom_call_target="tpu_custom_call" | custom-call | flops 436207616 | bytes 5669888 | tf_op jit(solution)/shard_map/pallas_call | solution.py:31
  100.5 1.9 collective-permute-start.4
  102.4 1.7 shard_map.114.keep_ref
  104.9 15.3 %all_to_all.37.got_ref = bf16[4,264,384]{2,1,0:T(8,128)(2,1)S(1)} all-to-all(bf16[4,264,384]{2,1,0:T(8,128)(2,1)S(1)} %shard_map.115), channel_id=1, replica_groups=mesh['x'=4,'z'=16,'y'=4,'c'=2] {'y'}, dimensions={0} | all-to-all | bytes 1622016 | tf_op jit(solution)/shard_map/all_to_all | solution.py:276
  121.0 14.2 %all_gather.7 = bf16[1056,384]{1,0:T(8,128)(2,1)S(1)} all-gather(bf16[264,384]{1,0:T(8,128)(2,1)S(1)} %get-tuple-element.27), channel_id=1, replica_groups=mesh['x'=4,'z'=16,'y'=4,'c'=2] {'y'}, dimensions={0}, use_global_device_ids=true | all-gather | bytes 1013760 | tf_op jit(solution)/shard_map/all_gather | solution.py:355
  135.2 1.9 collective-permute-start.5
  137.1 1.7 shard_map.117
  139.4 2.6 %shard_map.118 = (bf16[256,512]{1,0:T(8,128)(2,1)S(1)}, f32[1,512]{1,0:T(1,128)}, bf16[512,128]{1,0:T(8,128)(2,1)S(1)}) custom-call(f32[256,512]{1,0:T(8,128)S(1)} %get-tuple-element.28.part_ref, f32[8,256]{1,0:T(8,128)S(1)} %get-tuple-element.29.part_inner_ref, bf16[4,264,384]{2,1,0:T(8,128)(2,1)S(1)} %collective-permute-done.5.other_ref, ...), custom_call_target="tpu_custom_call" | custom-call | flops 436207616 | bytes 5680128 | tf_op jit(solution)/shard_map/pallas_call | solution.py:31
  142.1 26.7 %all_to_all.38.in_ref = bf16[16,32,128]{2,1,0:T(8,128)(2,1)S(1)} all-to-all(bf16[16,32,128]{2,1,0:T(8,128)(2,1)S(1)} %bitcast.13), channel_id=1, replica_groups=mesh['x'=4,'z'=16,'y'=4,'c'=2] {'z'}, dimensions={0} | all-to-all | bytes 262144 | tf_op jit(solution)/shard_map/all_to_all | solution.py:276
  168.8 10.4 %all_to_all.39.offset_ref = f32[4,32,128]{2,1,0:T(8,128)S(1)} all-to-all(f32[4,32,128]{2,1,0:T(8,128)S(1)} %shard_map.121), channel_id=1, replica_groups=mesh['x'=4,'z'=16,'y'=4,'c'=2] {'x'}, dimensions={0} | all-to-all | bytes 131072 | tf_op jit(solution)/shard_map/all_to_all | solution.py:276
  179.9 4.1 %all-to-all-start.6 = ((bf16[16,32,128]{2,1,0:T(8,128)(2,1)}), bf16[16,32,128]{2,1,0:T(8,128)(2,1)S(1)}, u32[]{:S(2)}, u32[]{:S(2)}) async-start(bf16[16,32,128]{2,1,0:T(8,128)(2,1)} %shard_map.122), calls=%async_computation.6 | async-start | bytes 262144 | tf_op jit(solution)/shard_map/all_to_all | solution.py:276
  184.0 0.9 copy-done.3
  187.1 0.9 copy-done.22
  188.0 1.9 shard_map.120
  190.8 1.0 copy-done.14
  191.8 3.0 %shard_map.124 = bf16[1,512,3072]{2,1,0:T(8,128)(2,1)} custom-call(bf16[4,264,384]{2,1,0:T(8,128)(2,1)S(1)} %bitcast.8, bf16[4,264,384]{2,1,0:T(8,128)(2,1)S(1)} %copy-done.12, f32[256,512]{1,0:T(8,128)S(1)} %copy-done.14, bf16[1,512]{1,0:T(2,128)(2,1)S(1)} %reshape.32.gain_ref, f32[8,256]{1,0:T(8,128)S(1)} %get-tuple-element.31.inverse_ref), custom_call_target="tpu_custom_call" | custom-call | flops 805306368 | bytes 5301248 | tf_op jit(solution)/shard_map/pallas_call | solution.py:31
  194.8 2.9 %all-to-all-done.6 = bf16[16,32,128]{2,1,0:T(8,128)(2,1)S(1)} async-done(((bf16[16,32,128]{2,1,0:T(8,128)(2,1)}), bf16[16,32,128]{2,1,0:T(8,128)(2,1)S(1)}, u32[]{:S(2)}, u32[]{:S(2)}) %all-to-all-start.6) | async-done | bytes 131104 | tf_op jit(solution)/shard_map/all_to_all | solution.py:276
  197.8 1.0 copy-done.20
  198.8 1.1 shard_map.123
  (60 shorter events, 10.8 us)
Async XLA Ops:
  0.6 91.2 %copy-start.2 = (bf16[256,512]{1,0:T(8,128)(2,1)S(1)}, bf16[256,512]{1,0:T(8,128)(2,1)}, u32[]{:S(2)}) copy-start(bf16[256,512]{1,0:T(8,128)(2,1)} %k_ref.7) | copy-start | bytes 786436
  0.6 91.2 %copy-start.24 = (bf16[512]{0:T(512)(128)(2,1)S(1)}, bf16[512]{0:T(512)(128)(2,1)}, u32[]{:S(2)}) copy-start(bf16[512]{0:T(512)(128)(2,1)} %param.9) | copy-start | bytes 3076
  0.7 91.2 %copy-start = (bf16[256,512]{1,0:T(8,128)(2,1)S(1)}, bf16[256,512]{1,0:T(8,128)(2,1)}, u32[]{:S(2)}) copy-start(bf16[256,512]{1,0:T(8,128)(2,1)} %q_ref.9) | copy-start | bytes 786436
  41.2 42.0 %collective-permute-start.1 = (bf16[768,512]{1,0:T(8,128)(2,1)S(1)}, bf16[768,512]{1,0:T(8,128)(2,1)S(1)}, u32[]{:S(2)}, u32[]{:S(2)}) collective-permute-start(bf16[768,512]{1,0:T(8,128)(2,1)S(1)} %all_gather.6.w0_ref), channel_id=1, source_target_pairs={{0,128},{128,256},{256,384},{384,0},{1,129},{129,257},{257,385},{3... | collective-permute-start | bytes 2359304 | tf_op jit(solution)/shard_map/ppermute | solution.py:311
  44.6 41.8 %collective-permute-start = (bf16[768,512]{1,0:T(8,128)(2,1)S(1)}, bf16[768,512]{1,0:T(8,128)(2,1)S(1)}, u32[]{:S(2)}, u32[]{:S(2)}) collective-permute-start(bf16[768,512]{1,0:T(8,128)(2,1)S(1)} %all_gather.6.w0_ref), channel_id=1, source_target_pairs={{0,384},{128,0},{256,128},{384,256},{1,385},{129,1},{257,129},{385... | collective-permute-start | bytes 2359304 | tf_op jit(solution)/shard_map/ppermute | solution.py:312
  48.3 1.0 copy-start.1
  49.2 0.9 copy-start.7
  79.1 17.1 %all-to-all-start.2 = ((bf16[16,32,128]{2,1,0:T(8,128)(2,1)}), bf16[16,32,128]{2,1,0:T(8,128)(2,1)S(1)}, u32[]{:S(2)}, u32[]{:S(2)}) async-start(bf16[16,32,128]{2,1,0:T(8,128)(2,1)} %shard_map.112), calls=%async_computation.2 | async-start | bytes 262144 | tf_op jit(solution)/shard_map/all_to_all | solution.py:276
  84.0 12.3 %collective-permute-start.2 = (bf16[384,512]{1,0:T(8,128)(2,1)}, bf16[384,512]{1,0:T(8,128)(2,1)S(1)}, u32[]{:S(2)}, u32[]{:S(2)}) collective-permute-start(bf16[384,512]{1,0:T(8,128)(2,1)} %slice.8), channel_id=1, source_target_pairs={{0,128},{128,256},{256,384},{384,0},{1,129},{129,257},{257,385},{3... | collective-permute-start | bytes 1179656 | tf_op jit(solution)/shard_map/ppermute | solution.py:313
  87.2 10.2 %collective-permute-start.3 = (bf16[384,512]{1,0:T(8,128)(2,1)}, bf16[384,512]{1,0:T(8,128)(2,1)}, u32[]{:S(2)}, u32[]{:S(2)}) collective-permute-start(bf16[384,512]{1,0:T(8,128)(2,1)} %slice.9), channel_id=1, source_target_pairs={{0,384},{128,0},{256,128},{384,256},{1,385},{129,1},{257,129},{385... | collective-permute-start | bytes 1179656 | tf_op jit(solution)/shard_map/ppermute | solution.py:314
  91.8 1.0 copy-start.8
  96.3 7.8 %copy-start.17 = (bf16[16,32,128]{2,1,0:T(8,128)(2,1)}, bf16[16,32,128]{2,1,0:T(8,128)(2,1)S(1)}, u32[]{:S(2)}) copy-start(bf16[16,32,128]{2,1,0:T(8,128)(2,1)S(1)} %all-to-all-done.2) | copy-start | bytes 393220
  96.3 7.8 %copy-start.5 = (bf16[384,512]{1,0:T(8,128)(2,1)}, bf16[384,512]{1,0:T(8,128)(2,1)S(1)}, u32[]{:S(2)}) copy-start(bf16[384,512]{1,0:T(8,128)(2,1)S(1)} %collective-permute-done.2.wa_ref) | copy-start | bytes 1179652
  97.4 1.0 copy-start.16
  100.5 39.0 %copy-start.13 = (f32[256,512]{1,0:T(8,128)}, f32[256,512]{1,0:T(8,128)S(1)}, u32[]{:S(2)}) copy-start(f32[256,512]{1,0:T(8,128)S(1)} %get-tuple-element.30.mixed_ref) | copy-start | bytes 1572868
  100.5 4.2 %collective-permute-start.4 = (bf16[4,264,384]{2,1,0:T(8,128)(2,1)S(1)}, bf16[4,264,384]{2,1,0:T(8,128)(2,1)S(1)}, u32[]{:S(2)}, u32[]{:S(2)}) collective-permute-start(bf16[4,264,384]{2,1,0:T(8,128)(2,1)S(1)} %get-tuple-element.24), channel_id=1, source_target_pairs={{0,1},{1,0},{2,3},{3,2},{4,5},{5,4},{6,7},{7,6},{8,9},{9,8},{10,11... | collective-permute-start | bytes 2433032 | tf_op jit(solution)/shard_map/ppermute | solution.py:339
  104.1 16.0 %copy-start.23 = (bf16[256,384]{1,0:T(8,128)(2,1)S(1)}, bf16[256,384]{1,0:T(8,128)(2,1)}, u32[]{:S(2)}) copy-start(bf16[256,384]{1,0:T(8,128)(2,1)} %target_ref.1) | copy-start | bytes 589828
  104.7 32.4 %copy-start.6 = (bf16[384,512]{1,0:T(8,128)(2,1)S(1)}, bf16[384,512]{1,0:T(8,128)(2,1)}, u32[]{:S(2)}) copy-start(bf16[384,512]{1,0:T(8,128)(2,1)} %copy-done.5) | copy-start | bytes 1179652
  135.2 4.2 %collective-permute-start.5 = (bf16[4,264,384]{2,1,0:T(8,128)(2,1)S(1)}, bf16[4,264,384]{2,1,0:T(8,128)(2,1)S(1)}, u32[]{:S(2)}, u32[]{:S(2)}) collective-permute-start(bf16[4,264,384]{2,1,0:T(8,128)(2,1)S(1)} %bitcast.6), channel_id=1, source_target_pairs={{0,1},{1,0},{2,3},{3,2},{4,5},{5,4},{6,7},{7,6},{8,9},{9,8},{10,11... | collective-permute-start | bytes 2433032 | tf_op jit(solution)/shard_map/ppermute | solution.py:356
  139.4 2.7 %copy-start.11 = (bf16[4,264,384]{2,1,0:T(8,128)(2,1)}, bf16[4,264,384]{2,1,0:T(8,128)(2,1)S(1)}, u32[]{:S(2)}) copy-start(bf16[4,264,384]{2,1,0:T(8,128)(2,1)S(1)} %collective-permute-done.5.other_ref) | copy-start | bytes 2433028
  142.1 26.7 %copy-start.21 = (bf16[256,512]{1,0:T(8,128)(2,1)}, bf16[256,512]{1,0:T(8,128)(2,1)S(1)}, u32[]{:S(2)}) copy-start(bf16[256,512]{1,0:T(8,128)(2,1)S(1)} %get-tuple-element.32.grad_ref) | copy-start | bytes 786436
  142.1 48.7 %copy-start.12 = (bf16[4,264,384]{2,1,0:T(8,128)(2,1)S(1)}, bf16[4,264,384]{2,1,0:T(8,128)(2,1)}, u32[]{:S(2)}) copy-start(bf16[4,264,384]{2,1,0:T(8,128)(2,1)} %copy-done.11) | copy-start | bytes 2433028
  179.9 17.9 %all-to-all-start.6 = ((bf16[16,32,128]{2,1,0:T(8,128)(2,1)}), bf16[16,32,128]{2,1,0:T(8,128)(2,1)S(1)}, u32[]{:S(2)}, u32[]{:S(2)}) async-start(bf16[16,32,128]{2,1,0:T(8,128)(2,1)} %shard_map.122), calls=%async_computation.6 | async-start | bytes 262144 | tf_op jit(solution)/shard_map/all_to_all | solution.py:276
  184.0 1.0 copy-start.3
  185.2 1.0 copy-start.9
  186.2 0.9 copy-start.18
  187.1 0.9 copy-start.22
  188.0 9.8 %copy-start.4 = (bf16[256,512]{1,0:T(8,128)(2,1)S(1)}, bf16[256,512]{1,0:T(8,128)(2,1)}, u32[]{:S(2)}) copy-start(bf16[256,512]{1,0:T(8,128)(2,1)} %k_ref.7) | copy-start | bytes 786436
  188.0 9.8 %copy-start.10 = (bf16[256,512]{1,0:T(8,128)(2,1)S(1)}, bf16[256,512]{1,0:T(8,128)(2,1)}, u32[]{:S(2)}) copy-start(bf16[256,512]{1,0:T(8,128)(2,1)} %v_ref.5) | copy-start | bytes 786436
  190.0 0.8 copy-start.19
  190.8 1.0 copy-start.14
  197.8 1.0 copy-start.20
  (1 other events, 0.8 us)
where the time goes:
time: 202 us; the launch traced here: 200 us
  blocking collectives  135 us (67%)
  starting transfers between devices  26 us (13%)
  Pallas kernels  17.8 us (9%)
  local copies, waits for them, and re-layouts  12.9 us (6%)
  waiting for transfers between devices  7.17 us (4%)
    all_to_all x5, blocking collectives, exchanged(): return lax.all_to_all(blocks, axis, 0, 0, tiled=True)  80.3 us
    all_gather x1, blocking collectives, work(): w0 = lax.all_gather(out_weight.T, 'z', axis=0, tiled=True)  40.5 us
    pallas_call x16, Pallas kernels, call(): pl.pallas_call(kernel, out_shape=outs, in_specs=[pl.BlockSpec(memory_spac...  17.8 us
    all_gather x1, blocking collectives, work(): own = lax.all_gather(grad_local, 'y', axis=0, tiled=True).reshape(message)  14.2 us
    unnamed x50, local copies, waits for them, and re-layouts  11.4 us
    all_to_all x2, starting transfers between devices, exchanged(): return lax.all_to_all(blocks, axis, 0, 0, tiled=True)  8.14 us
    all_to_all x2, waiting for transfers between devices, exchanged(): return lax.all_to_all(blocks, axis, 0, 0, tiled=True)  4.99 us
    ppermute x1, starting transfers between devices, work(): wb = lax.ppermute(w1[width:], 'x', ring(NX, -1))  4.57 us
  transfers between devices with their start and end apart: 8, of which 5 were waited for; matrix products, arithmetic and copies ran while one was open for 1% of the time, Pallas kernels for 5%

commit v1 on v0

--- a/solution.py
+++ b/solution.py
@@ -25,7 +25,7 @@
     return lax.dot_general(a, b, (((ca,), (cb,)), ((), ())), preferred_element_type=F32)
 
 
-def call(kernel, outs, args, flops=0):
+def call(kernel, outs, args, flops=0, vmem=VMEM_LIMIT):
     moved = sum(a.size * a.dtype.itemsize for a in args)
     moved += sum(o.size * o.dtype.itemsize for o in outs)
     return pl.pallas_call(
@@ -34,7 +34,7 @@
         in_specs=[pl.BlockSpec(memory_space=pltpu.VMEM)] * len(args),
         out_specs=[pl.BlockSpec(memory_space=pltpu.VMEM)] * len(outs),
         cost_estimate=pl.CostEstimate(flops=flops, bytes_accessed=moved, transcendentals=0),
-        compiler_params=pltpu.CompilerParams(vmem_limit_bytes=VMEM_LIMIT),
+        compiler_params=pltpu.CompilerParams(vmem_limit_bytes=vmem),
     )(*args)
 
 
@@ -241,13 +241,13 @@
 
 
 def local_grad_kernel(
-    q_ref, k_ref, v_ref, grad_ref, state_ref, scores_ref, query_ref, key_ref, value_ref
+    q_ref, k_ref, v_ref, grad_ref, state_ref, query_ref, key_ref, value_ref
 ):
     keep = keep_mask(q_ref.shape[0])
     for h in range(q_ref.shape[1] // HEAD_DIM):
         cols = head_cols(h)
         q, k, v, grad = q_ref[:, cols], k_ref[:, cols], v_ref[:, cols], grad_ref[:, cols]
-        scores = scores_ref[h]
+        scores = jnp.where(keep, dot(q, k, 1, 1), 0.0).astype(BF16)
         pairs = jnp.where(keep, dot(grad, v, 1, 1), 0.0).astype(BF16)
         query = dot(pairs, k, 1, 0) + dot(grad, state_ref[cols, :], 1, 1)
         query_ref[:, cols] = query.astype(BF16)
@@ -262,14 +262,6 @@
         key_ref[:, cols] = (key_part_ref[:, cols] + dot(v_ref[:, cols], later, 1, 1)).astype(BF16)
         value = value_part_ref[:, cols] + dot(k_ref[:, cols], later, 1, 0)
         value_ref[:, cols] = value.astype(BF16)
-
-
-def scores_kernel(q_ref, k_ref, out_ref):
-    keep = keep_mask(q_ref.shape[0])
-    for h in range(q_ref.shape[1] // HEAD_DIM):
-        cols = head_cols(h)
-        scores = dot(q_ref[:, cols], k_ref[:, cols], 1, 1)
-        out_ref[h] = jnp.where(keep, scores, 0.0).astype(BF16)
 
 
 def exchanged(blocks, axis):
@@ -339,10 +331,6 @@
     got = lax.ppermute(sent, "c", swap)
     (paired,) = call(pair_kernel, [arr(message, BF16)], [kept, got, sums])
     arrived = exchanged(paired, "y")
-    (scores,) = call(
-        scores_kernel, [arr((feats // HEAD_DIM, count, count), BF16)], [queries, key_input],
-        mm * count,
-    )
     output, grad_local, inverse = call(
         output_kernel,
         [
@@ -367,13 +355,13 @@
     )
     (weight_grads,) = call(
         weight_grad_kernel, [arr((1, feats, columns), BF16)],
-        [own, other, mixed, gain, inverse], mm * columns,
+        [own, other, mixed, gain, inverse], mm * columns, 60 << 20,
     )
     query_grad, key_part, value_part = call(
         local_grad_kernel,
         [arr((count, feats), BF16), arr((count, feats), F32), arr((count, feats), F32)],
-        [queries, key_input, value_input, mixed_grad, state_low, scores],
-        mm * (4 * count + HEAD_DIM),
+        [queries, key_input, value_input, mixed_grad, state_low],
+        mm * (5 * count + HEAD_DIM), 60 << 20,
     )
     later_low = carried(grad_state, True)
     key_grad, value_grad = call(

time: 202 us -> 200 us (0.990)
  local copies, waits for them, and re-layouts: 12.9 us -> 8.1 us
  waiting for transfers between devices: 7.17 us -> 10.7 us
    unnamed x50 -> x46, local copies, waits for them, and re-layouts: 11.4 us -> 6.53 us
    pallas_call x16 -> x15, Pallas kernels: 17.8 us -> 17.6 us  [call(): pl.pallas_call(kernel, out_shape=outs, in_specs=[pl.BlockSpec(memory_spac...]
  transfers between devices with their start and end apart: 8 -> 8, of which waited for: 5 -> 5; matrix products, arithmetic and copies ran while one was open for 1% -> 1% of each run, Pallas kernels for 5% -> 6%
where the time goes in v1:
time: 200 us; the launch traced here: 198 us
  blocking collectives  135 us (68%)
  starting transfers between devices  26.2 us (13%)
  Pallas kernels  17.6 us (9%)
  waiting for transfers between devices  10.7 us (5%)
  local copies, waits for them, and re-layouts  8.1 us (4%)
    all_to_all x5, blocking collectives, exchanged(): return lax.all_to_all(blocks, axis, 0, 0, tiled=True)  80.1 us
    all_gather x1, blocking collectives, work(): w0 = lax.all_gather(out_weight.T, 'z', axis=0, tiled=True)  40.5 us
    pallas_call x15, Pallas kernels, call(): pl.pallas_call(kernel, out_shape=outs, in_specs=[pl.BlockSpec(memory_spac...  17.6 us
    all_gather x1, blocking collectives, work(): own = lax.all_gather(grad_local, 'y', axis=0, tiled=True).reshape(message)  14.2 us
    all_to_all x2, starting transfers between devices, exchanged(): return lax.all_to_all(blocks, axis, 0, 0, tiled=True)  8.27 us
    unnamed x46, local copies, waits for them, and re-layouts  6.53 us
    all_to_all x2, waiting for transfers between devices, exchanged(): return lax.all_to_all(blocks, axis, 0, 0, tiled=True)  6.52 us
    ppermute x1, starting transfers between devices, work(): wb = lax.ppermute(w1[width:], 'x', ring(NX, -1))  4.57 us
  transfers between devices with their start and end apart: 8, of which 5 were waited for; matrix products, arithmetic and copies ran while one was open for 1% of the time, Pallas kernels for 6%

profile of v1, /device:TPU:24, one launch (start us, length us, event | category | flops | bytes accessed | tf_op | source)
XLA Modules:
  0.0 198.3 jit_solution(2052272142477325089)
XLA Ops:
  0.7 40.5 %all_gather.6.w0_ref = bf16[768,512]{1,0:T(8,128)(2,1)S(1)} all-gather(bf16[48,512]{1,0:T(8,128)(2,1)} %bitcast.12), channel_id=1, replica_groups=mesh['x'=4,'z'=16,'y'=4,'c'=2] {'z'}, dimensions={0}, use_global_device_ids=true | all-gather | bytes 835584 | tf_op jit(solution)/shard_map/all_gather | solution.py:302
  41.2 3.4 %collective-permute-start.1 = (bf16[768,512]{1,0:T(8,128)(2,1)S(1)}, bf16[768,512]{1,0:T(8,128)(2,1)S(1)}, u32[]{:S(2)}, u32[]{:S(2)}) collective-permute-start(bf16[768,512]{1,0:T(8,128)(2,1)S(1)} %all_gather.6.w0_ref), channel_id=1, source_target_pairs={{0,128},{128,256},{256,384},{384,0},{1,129},{129,257},{257,385},{3... | collective-permute-start | bytes 2359304 | tf_op jit(solution)/shard_map/ppermute | solution.py:303
  44.6 3.7 %collective-permute-start = (bf16[768,512]{1,0:T(8,128)(2,1)S(1)}, bf16[768,512]{1,0:T(8,128)(2,1)S(1)}, u32[]{:S(2)}, u32[]{:S(2)}) collective-permute-start(bf16[768,512]{1,0:T(8,128)(2,1)S(1)} %all_gather.6.w0_ref), channel_id=1, source_target_pairs={{0,384},{128,0},{256,128},{384,256},{1,385},{129,1},{257,129},{385... | collective-permute-start | bytes 2359304 | tf_op jit(solution)/shard_map/ppermute | solution.py:304
  48.3 0.9 copy-done.7
  49.2 0.9 copy-done.10
  50.4 19.5 %all_to_all.35.in_ref = bf16[16,32,128]{2,1,0:T(8,128)(2,1)S(1)} all-to-all(bf16[16,32,128]{2,1,0:T(8,128)(2,1)S(1)} %bitcast.9), channel_id=1, replica_groups=mesh['x'=4,'z'=16,'y'=4,'c'=2] {'z'}, dimensions={0} | all-to-all | bytes 262144 | tf_op jit(solution)/shard_map/all_to_all | solution.py:268
  69.9 8.5 %all_to_all.36.offset_ref = f32[4,32,128]{2,1,0:T(8,128)S(1)} all-to-all(f32[4,32,128]{2,1,0:T(8,128)S(1)} %shard_map.111), channel_id=1, replica_groups=mesh['x'=4,'z'=16,'y'=4,'c'=2] {'x'}, dimensions={0} | all-to-all | bytes 131072 | tf_op jit(solution)/shard_map/all_to_all | solution.py:268
  79.1 4.2 %all-to-all-start.2 = ((bf16[16,32,128]{2,1,0:T(8,128)(2,1)}), bf16[16,32,128]{2,1,0:T(8,128)(2,1)}, u32[]{:S(2)}, u32[]{:S(2)}) async-start(bf16[16,32,128]{2,1,0:T(8,128)(2,1)} %shard_map.112), calls=%async_computation.2 | async-start | bytes 262144 | tf_op jit(solution)/shard_map/all_to_all | solution.py:268
  84.1 2.5 %collective-permute-start.2 = (bf16[384,512]{1,0:T(8,128)(2,1)}, bf16[384,512]{1,0:T(8,128)(2,1)S(1)}, u32[]{:S(2)}, u32[]{:S(2)}) collective-permute-start(bf16[384,512]{1,0:T(8,128)(2,1)} %slice.8), channel_id=1, source_target_pairs={{0,128},{128,256},{256,384},{384,0},{1,129},{129,257},{257,385},{3... | collective-permute-start | bytes 1179656 | tf_op jit(solution)/shard_map/ppermute | solution.py:305
  86.6 0.8 slice.9
  87.4 4.6 %collective-permute-start.3 = (bf16[384,512]{1,0:T(8,128)(2,1)}, bf16[384,512]{1,0:T(8,128)(2,1)S(1)}, u32[]{:S(2)}, u32[]{:S(2)}) collective-permute-start(bf16[384,512]{1,0:T(8,128)(2,1)} %slice.9), channel_id=1, source_target_pairs={{0,384},{128,0},{256,128},{384,256},{1,385},{129,1},{257,129},{385... | collective-permute-start | bytes 1179656 | tf_op jit(solution)/shard_map/ppermute | solution.py:306
  92.0 0.9 copy-done.8
  92.9 0.9 copy-done.11
  95.3 1.1 all-to-all-done.2
  96.4 1.1 collective-permute-done.3.wb_ref
  97.5 1.2 copy-done.15
  98.7 1.9 shard_map.113
  100.7 1.9 collective-permute-start.4
  103.3 1.5 collective-permute-done.4.got_ref
  105.1 15.4 %all_to_all.37.got_ref = bf16[4,264,384]{2,1,0:T(8,128)(2,1)S(1)} all-to-all(bf16[4,264,384]{2,1,0:T(8,128)(2,1)S(1)} %shard_map.115), channel_id=1, replica_groups=mesh['x'=4,'z'=16,'y'=4,'c'=2] {'y'}, dimensions={0} | all-to-all | bytes 1622016 | tf_op jit(solution)/shard_map/all_to_all | solution.py:268
  120.5 0.9 shard_map.116
  121.4 14.2 %all_gather.7 = bf16[1056,384]{1,0:T(8,128)(2,1)S(1)} all-gather(bf16[264,384]{1,0:T(8,128)(2,1)S(1)} %get-tuple-element.27), channel_id=1, replica_groups=mesh['x'=4,'z'=16,'y'=4,'c'=2] {'y'}, dimensions={0}, use_global_device_ids=true | all-gather | bytes 1013760 | tf_op jit(solution)/shard_map/all_gather | solution.py:343
  135.5 1.9 collective-permute-start.5
  138.2 1.5 collective-permute-done.5.other_ref
  139.7 1.4 shard_map.118
  141.9 26.4 %all_to_all.38.in_ref = bf16[16,32,128]{2,1,0:T(8,128)(2,1)S(1)} all-to-all(bf16[16,32,128]{2,1,0:T(8,128)(2,1)S(1)} %bitcast.11), channel_id=1, replica_groups=mesh['x'=4,'z'=16,'y'=4,'c'=2] {'z'}, dimensions={0} | all-to-all | bytes 262144 | tf_op jit(solution)/shard_map/all_to_all | solution.py:268
  168.3 10.3 %all_to_all.39.offset_ref = f32[4,32,128]{2,1,0:T(8,128)S(1)} all-to-all(f32[4,32,128]{2,1,0:T(8,128)S(1)} %shard_map.120), channel_id=1, replica_groups=mesh['x'=4,'z'=16,'y'=4,'c'=2] {'x'}, dimensions={0} | all-to-all | bytes 131072 | tf_op jit(solution)/shard_map/all_to_all | solution.py:268
  179.3 4.1 %all-to-all-start.6 = ((bf16[16,32,128]{2,1,0:T(8,128)(2,1)}), bf16[16,32,128]{2,1,0:T(8,128)(2,1)S(1)}, u32[]{:S(2)}, u32[]{:S(2)}) async-start(bf16[16,32,128]{2,1,0:T(8,128)(2,1)} %shard_map.121), calls=%async_computation.6 | async-start | bytes 262144 | tf_op jit(solution)/shard_map/all_to_all | solution.py:268
  183.4 3.7 %shard_map.119 = (bf16[256,512]{1,0:T(8,128)(2,1)}, f32[256,512]{1,0:T(8,128)}, f32[256,512]{1,0:T(8,128)}) custom-call(bf16[256,512]{1,0:T(8,128)(2,1)} %q_ref.7, bf16[256,512]{1,0:T(8,128)(2,1)} %k_ref.5, bf16[256,512]{1,0:T(8,128)(2,1)} %v_ref.5, bf16[256,512]{1,0:T(8,128)(2,1)} %copy-done.21, bf16[512,128]{1,0:T(8,128)(2,1)} %bitcast.1.state_ref), custom_call_target="tpu_custom_call" | custom-call | flops 369098752 | bytes 2490368 | tf_op jit(solution)/shard_map/pallas_call | solution.py:31
  187.1 4.7 %shard_map.123 = bf16[1,512,3072]{2,1,0:T(8,128)(2,1)} custom-call(bf16[4,264,384]{2,1,0:T(8,128)(2,1)} %bitcast.8, bf16[4,264,384]{2,1,0:T(8,128)(2,1)} %copy-done.5, f32[256,512]{1,0:T(8,128)} %copy-done.13, bf16[1,512]{1,0:T(2,128)(2,1)} %copy-done.19, f32[8,256]{1,0:T(8,128)} %copy-done.20), custom_call_target="tpu_custom_call" | custom-call | flops 805306368 | bytes 5301248 | tf_op jit(solution)/shard_map/pallas_call | solution.py:31
  191.8 5.4 %all-to-all-done.6 = bf16[16,32,128]{2,1,0:T(8,128)(2,1)S(1)} async-done(((bf16[16,32,128]{2,1,0:T(8,128)(2,1)}), bf16[16,32,128]{2,1,0:T(8,128)(2,1)S(1)}, u32[]{:S(2)}, u32[]{:S(2)}) %all-to-all-start.6) | async-done | bytes 131104 | tf_op jit(solution)/shard_map/all_to_all | solution.py:268
  197.2 1.1 shard_map.122
  (55 shorter events, 6.3 us)
Async XLA Ops:
  0.6 91.3 %copy-start.22 = (bf16[512]{0:T(512)(128)(2,1)S(1)}, bf16[512]{0:T(512)(128)(2,1)}, u32[]{:S(2)}) copy-start(bf16[512]{0:T(512)(128)(2,1)} %param.9) | copy-start | bytes 3076
  0.6 91.3 %copy-start.6 = (bf16[256,512]{1,0:T(8,128)(2,1)S(1)}, bf16[256,512]{1,0:T(8,128)(2,1)}, u32[]{:S(2)}) copy-start(bf16[256,512]{1,0:T(8,128)(2,1)} %q_ref.7) | copy-start | bytes 786436
  41.2 42.1 %collective-permute-start.1 = (bf16[768,512]{1,0:T(8,128)(2,1)S(1)}, bf16[768,512]{1,0:T(8,128)(2,1)S(1)}, u32[]{:S(2)}, u32[]{:S(2)}) collective-permute-start(bf16[768,512]{1,0:T(8,128)(2,1)S(1)} %all_gather.6.w0_ref), channel_id=1, source_target_pairs={{0,128},{128,256},{256,384},{384,0},{1,129},{129,257},{257,385},{3... | collective-permute-start | bytes 2359304 | tf_op jit(solution)/shard_map/ppermute | solution.py:303
  44.6 42.0 %collective-permute-start = (bf16[768,512]{1,0:T(8,128)(2,1)S(1)}, bf16[768,512]{1,0:T(8,128)(2,1)S(1)}, u32[]{:S(2)}, u32[]{:S(2)}) collective-permute-start(bf16[768,512]{1,0:T(8,128)(2,1)S(1)} %all_gather.6.w0_ref), channel_id=1, source_target_pairs={{0,384},{128,0},{256,128},{384,256},{1,385},{129,1},{257,129},{385... | collective-permute-start | bytes 2359304 | tf_op jit(solution)/shard_map/ppermute | solution.py:304
  48.3 1.0 copy-start.7
  49.2 0.9 copy-start.10
  79.1 17.3 %all-to-all-start.2 = ((bf16[16,32,128]{2,1,0:T(8,128)(2,1)}), bf16[16,32,128]{2,1,0:T(8,128)(2,1)}, u32[]{:S(2)}, u32[]{:S(2)}) async-start(bf16[16,32,128]{2,1,0:T(8,128)(2,1)} %shard_map.112), calls=%async_computation.2 | async-start | bytes 262144 | tf_op jit(solution)/shard_map/all_to_all | solution.py:268
  84.1 12.3 %collective-permute-start.2 = (bf16[384,512]{1,0:T(8,128)(2,1)}, bf16[384,512]{1,0:T(8,128)(2,1)S(1)}, u32[]{:S(2)}, u32[]{:S(2)}) collective-permute-start(bf16[384,512]{1,0:T(8,128)(2,1)} %slice.8), channel_id=1, source_target_pairs={{0,128},{128,256},{256,384},{384,0},{1,129},{129,257},{257,385},{3... | collective-permute-start | bytes 1179656 | tf_op jit(solution)/shard_map/ppermute | solution.py:305
  87.4 10.2 %collective-permute-start.3 = (bf16[384,512]{1,0:T(8,128)(2,1)}, bf16[384,512]{1,0:T(8,128)(2,1)S(1)}, u32[]{:S(2)}, u32[]{:S(2)}) collective-permute-start(bf16[384,512]{1,0:T(8,128)(2,1)} %slice.9), channel_id=1, source_target_pairs={{0,384},{128,0},{256,128},{384,256},{1,385},{129,1},{257,129},{385... | collective-permute-start | bytes 1179656 | tf_op jit(solution)/shard_map/ppermute | solution.py:306
  92.0 1.0 copy-start.8
  92.9 0.9 copy-start.11
  93.9 45.9 %copy-start.19 = (bf16[1,512]{1,0:T(2,128)(2,1)}, bf16[1,512]{1,0:T(2,128)(2,1)S(1)}, u32[]{:S(2)}) copy-start(bf16[1,512]{1,0:T(2,128)(2,1)S(1)} %reshape.32.gain_ref) | copy-start | bytes 3076
  94.5 0.8 copy-start.14
  96.4 6.9 %copy-start.1 = (bf16[384,512]{1,0:T(8,128)(2,1)}, bf16[384,512]{1,0:T(8,128)(2,1)S(1)}, u32[]{:S(2)}) copy-start(bf16[384,512]{1,0:T(8,128)(2,1)S(1)} %collective-permute-done.2.wa_ref) | copy-start | bytes 1179652
  97.5 5.8 %copy-start.3 = (bf16[384,512]{1,0:T(8,128)(2,1)}, bf16[384,512]{1,0:T(8,128)(2,1)S(1)}, u32[]{:S(2)}) copy-start(bf16[384,512]{1,0:T(8,128)(2,1)S(1)} %collective-permute-done.3.wb_ref) | copy-start | bytes 1179652
  97.5 1.2 copy-start.15
  100.6 39.1 %copy-start.13 = (f32[256,512]{1,0:T(8,128)}, f32[256,512]{1,0:T(8,128)S(1)}, u32[]{:S(2)}) copy-start(f32[256,512]{1,0:T(8,128)S(1)} %get-tuple-element.30.mixed_ref) | copy-start | bytes 1572868
  100.7 4.2 %collective-permute-start.4 = (bf16[4,264,384]{2,1,0:T(8,128)(2,1)S(1)}, bf16[4,264,384]{2,1,0:T(8,128)(2,1)S(1)}, u32[]{:S(2)}, u32[]{:S(2)}) collective-permute-start(bf16[4,264,384]{2,1,0:T(8,128)(2,1)S(1)} %get-tuple-element.24), channel_id=1, source_target_pairs={{0,1},{1,0},{2,3},{3,2},{4,5},{5,4},{6,7},{7,6},{8,9},{9,8},{10,11... | collective-permute-start | bytes 2433032 | tf_op jit(solution)/shard_map/ppermute | solution.py:331
  103.3 17.1 %copy-start.18 = (bf16[256,384]{1,0:T(8,128)(2,1)S(1)}, bf16[256,384]{1,0:T(8,128)(2,1)}, u32[]{:S(2)}) copy-start(bf16[256,384]{1,0:T(8,128)(2,1)} %target_ref.1) | copy-start | bytes 589828
  104.9 32.6 %copy-start.2 = (bf16[384,512]{1,0:T(8,128)(2,1)S(1)}, bf16[384,512]{1,0:T(8,128)(2,1)}, u32[]{:S(2)}) copy-start(bf16[384,512]{1,0:T(8,128)(2,1)} %copy-done.1) | copy-start | bytes 1179652
  104.9 32.6 %copy-start.4 = (bf16[384,512]{1,0:T(8,128)(2,1)S(1)}, bf16[384,512]{1,0:T(8,128)(2,1)}, u32[]{:S(2)}) copy-start(bf16[384,512]{1,0:T(8,128)(2,1)} %copy-done.3) | copy-start | bytes 1179652
  121.4 19.8 %copy-start.20 = (f32[8,256]{1,0:T(8,128)}, f32[8,256]{1,0:T(8,128)S(1)}, u32[]{:S(2)}) copy-start(f32[8,256]{1,0:T(8,128)S(1)} %get-tuple-element.31.inverse_ref) | copy-start | bytes 24580
  135.5 5.6 %copy-start = (bf16[1056,384]{1,0:T(8,128)(2,1)}, bf16[1056,384]{1,0:T(8,128)(2,1)S(1)}, u32[]{:S(2)}) copy-start(bf16[1056,384]{1,0:T(8,128)(2,1)S(1)} %all_gather.7) | copy-start | bytes 2433028
  135.5 4.2 %collective-permute-start.5 = (bf16[4,264,384]{2,1,0:T(8,128)(2,1)S(1)}, bf16[4,264,384]{2,1,0:T(8,128)(2,1)S(1)}, u32[]{:S(2)}, u32[]{:S(2)}) collective-permute-start(bf16[4,264,384]{2,1,0:T(8,128)(2,1)S(1)} %bitcast.6), channel_id=1, source_target_pairs={{0,1},{1,0},{2,3},{3,2},{4,5},{5,4},{6,7},{7,6},{8,9},{9,8},{10,11... | collective-permute-start | bytes 2433032 | tf_op jit(solution)/shard_map/ppermute | solution.py:344
  139.7 2.1 %copy-start.5 = (bf16[4,264,384]{2,1,0:T(8,128)(2,1)}, bf16[4,264,384]{2,1,0:T(8,128)(2,1)S(1)}, u32[]{:S(2)}) copy-start(bf16[4,264,384]{2,1,0:T(8,128)(2,1)S(1)} %collective-permute-done.5.other_ref) | copy-start | bytes 2433028
  141.2 0.7 copy-start.21
  179.3 17.9 %all-to-all-start.6 = ((bf16[16,32,128]{2,1,0:T(8,128)(2,1)}), bf16[16,32,128]{2,1,0:T(8,128)(2,1)S(1)}, u32[]{:S(2)}, u32[]{:S(2)}) async-start(bf16[16,32,128]{2,1,0:T(8,128)(2,1)} %shard_map.121), calls=%async_computation.6 | async-start | bytes 262144 | tf_op jit(solution)/shard_map/all_to_all | solution.py:268
  183.4 13.8 %copy-start.9 = (bf16[256,512]{1,0:T(8,128)(2,1)S(1)}, bf16[256,512]{1,0:T(8,128)(2,1)}, u32[]{:S(2)}) copy-start(bf16[256,512]{1,0:T(8,128)(2,1)} %k_ref.5) | copy-start | bytes 786436
  183.4 13.8 %copy-start.12 = (bf16[256,512]{1,0:T(8,128)(2,1)S(1)}, bf16[256,512]{1,0:T(8,128)(2,1)}, u32[]{:S(2)}) copy-start(bf16[256,512]{1,0:T(8,128)(2,1)} %v_ref.5) | copy-start | bytes 786436
  187.1 10.1 %copy-start.16 = (f32[256,512]{1,0:T(8,128)S(1)}, f32[256,512]{1,0:T(8,128)}, u32[]{:S(2)}) copy-start(f32[256,512]{1,0:T(8,128)} %get-tuple-element.34.key_part_ref) | copy-start | bytes 1572868
  187.1 10.1 %copy-start.17 = (f32[256,512]{1,0:T(8,128)S(1)}, f32[256,512]{1,0:T(8,128)}, u32[]{:S(2)}) copy-start(f32[256,512]{1,0:T(8,128)} %get-tuple-element.35.value_part_ref) | copy-start | bytes 1572868

commit v2 on v1

--- a/solution.py
+++ b/solution.py
@@ -1,5 +1,3 @@
-import functools
-
 import jax
 import jax.numpy as jnp
 from jax import lax
@@ -11,12 +9,15 @@
 
 HEAD_DIM = 128
 FEATURES = 4096
-SEQ = ("x", "z")
+SEQ = ("x", "zh", "zl")
+Z = ("zh", "zl")
+NEAR = ("x", "zl")
 HEAD = ("y", "c")
 EPSILON = 1e-06
 F32 = jnp.float32
 BF16 = jnp.bfloat16
 NX, NZ, NY, NC = 4, 16, 4, 2
+FAR = 4
 VMEM_LIMIT = 16 << 20
 EXTRA = 8
 
@@ -90,22 +91,20 @@
         out_ref[:, cols] = dot(scores, v_ref[:, cols], 1, 0)
 
 
-def totals_kernel(reverse, in_ref, out_ref):
+def totals_kernel(in_ref, out_ref):
     total = in_ref[0].astype(F32)
     for i in range(1, NZ):
         total = total + in_ref[i].astype(F32)
     x = lax.axis_index("x")
     for k in range(NX):
-        sent = (k < x) if reverse else (k > x)
-        out_ref[k] = jnp.where(sent, total, 0.0)
-
-
-def prefix_kernel(reverse, in_ref, offset_ref, out_ref):
+        out_ref[k] = jnp.where(k > x, total, 0.0)
+
+
+def prefix_kernel(in_ref, offset_ref, out_ref):
     running = offset_ref[0]
     for k in range(1, NX):
         running = running + offset_ref[k]
-    order = range(NZ)
-    for i in reversed(order) if reverse else order:
+    for i in range(NZ):
         out_ref[i] = running.astype(BF16)
         running = running + in_ref[i].astype(F32)
 
@@ -121,6 +120,33 @@
         (lambda: jnp.where(c == 0, first, second), lambda: jnp.where(c == 0, second, first)),
         (lambda: w3_ref[own, :], lambda: w3_ref[other, :]),
     )
+
+
+def group_totals_kernel(in_ref, out_ref):
+    near = NZ // FAR
+    rows = in_ref.shape[1]
+    for x in range(NX):
+        total = in_ref[x * near].astype(F32)
+        for i in range(1, near):
+            total = total + in_ref[x * near + i].astype(F32)
+        for k in range(FAR):
+            out_ref[k, x * rows : (x + 1) * rows, :] = total.astype(BF16)
+
+
+def suffix_kernel(in_ref, groups_ref, out_ref):
+    near = NZ // FAR
+    rows = in_ref.shape[1]
+    me = lax.axis_index("zh")
+    carry = jnp.zeros(in_ref.shape[1:], F32)
+    for x in reversed(range(NX)):
+        running = carry
+        for k in range(FAR):
+            group = groups_ref[k, x * rows : (x + 1) * rows, :].astype(F32)
+            running = running + jnp.where(k > me, group, 0.0)
+            carry = carry + group
+        for i in reversed(range(near)):
+            out_ref[x * near + i] = running.astype(BF16)
+            running = running + in_ref[x * near + i].astype(F32)
 
 
 def project_kernel(
@@ -183,13 +209,13 @@
 
 
 def normed_grad_kernel(
-    core, grad_ref, w0_ref, w1_ref, w3_ref, wa_ref, wb_ref, out_ref, inner_ref
+    grad_ref, w0_ref, w1_ref, w3_ref, wa_ref, wb_ref, out_ref, inner_ref
 ):
     count, width = out_ref.shape[0], grad_ref.shape[2]
     x, c = lax.axis_index("x"), lax.axis_index("c")
     total = None
     for r, pair in enumerate(halves((w0_ref, w1_ref, w3_ref, wa_ref, wb_ref), c, width)):
-        part = dot(grad_ref[lax.rem(x + r, NX), 0:count, :], pair[core](), 1, 0)
+        part = dot(grad_ref[lax.rem(x + r, NX), 0:count, :], pair[0](), 1, 0)
         total = part if total is None else total + part
     out_ref[...] = total
     inner = unpack_rows(grad_ref[0, count : count + EXTRA, 0:count])
@@ -268,20 +294,30 @@
     return lax.all_to_all(blocks, axis, 0, 0, tiled=True)
 
 
-def carried(state, reverse):
+def carried(state):
     rows, cols = state.shape
     blocks = state.reshape(NZ, rows // NZ, cols)
-    got = exchanged(blocks, "z")
+    got = exchanged(blocks, Z)
     (totals,) = call(
-        functools.partial(totals_kernel, reverse),
+        totals_kernel,
         [arr((NX, rows // NZ, cols), F32)], [got],
     )
     offsets = exchanged(totals, "x")
     (sums,) = call(
-        functools.partial(prefix_kernel, reverse),
+        prefix_kernel,
         [arr(blocks.shape, BF16)], [got, offsets],
     )
-    return exchanged(sums, "z").reshape(rows, cols)
+    return exchanged(sums, Z).reshape(rows, cols)
+
+
+def carried_back(state):
+    rows, cols = state.shape
+    blocks = state.reshape(NZ, rows // NZ, cols)
+    got = exchanged(blocks, NEAR)
+    (totals,) = call(group_totals_kernel, [arr((FAR, NX * (rows // NZ), cols), BF16)], [got])
+    groups = exchanged(totals, "zh")
+    (sums,) = call(suffix_kernel, [arr(blocks.shape, BF16)], [got, groups])
+    return exchanged(sums, NEAR).reshape(rows, cols)
 
 
 def ring(count, step):
@@ -297,9 +333,9 @@
 
     (state_local,) = call(
         state_kernel, [arr((feats, HEAD_DIM), BF16)], [key_input, value_input],
-        mm * HEAD_DIM,
-    )
-    w0 = lax.all_gather(out_weight.T, "z", axis=0, tiled=True)
+        mm * HEAD_DIM, 60 << 20,
+    )
+    w0 = lax.all_gather(out_weight.T, Z, axis=0, tiled=True)
     w3 = lax.ppermute(w0, "x", ring(NX, 1))
     w1 = lax.ppermute(w0, "x", ring(NX, -1))
     wa = lax.ppermute(w3[:width], "x", ring(NX, 1))
@@ -308,9 +344,9 @@
 
     (attended,) = call(
         local_kernel, [arr((count, feats), F32)], [queries, key_input, value_input],
-        2 * mm * count,
-    )
-    state_low = carried(state_local, False)
+        2 * mm * count, 60 << 20,
+    )
+    state_low = carried(state_local)
     message = (NY, count + EXTRA, width)
     columns = NY * NC * width
     mixed, scaled, sent, sums = call(
@@ -343,7 +379,7 @@
     own = lax.all_gather(grad_local, "y", axis=0, tiled=True).reshape(message)
     other = lax.ppermute(own, "c", swap)
     part, part_inner = call(
-        functools.partial(normed_grad_kernel, 0),
+        normed_grad_kernel,
         [arr((count, feats), F32), arr((EXTRA, count), F32)], [own, *weights],
         mm * columns // 2,
     )
@@ -363,7 +399,7 @@
         [queries, key_input, value_input, mixed_grad, state_low],
         mm * (5 * count + HEAD_DIM), 60 << 20,
     )
-    later_low = carried(grad_state, True)
+    later_low = carried_back(grad_state)
     key_grad, value_grad = call(
         later_kernel, [arr((count, feats), BF16)] * 2,
         [key_input, value_input, key_part, value_part, later_low], 2 * mm * HEAD_DIM,
@@ -372,7 +408,7 @@
 
 
 def solution(mesh):
-    torus = Mesh(mesh.devices.reshape(NX, NZ, NY, NC), ("x", "z", "y", "c"))
+    torus = Mesh(mesh.devices.reshape(NX, FAR, NZ // FAR, NY, NC), ("x", "zh", "zl", "y", "c"))
     return jax.shard_map(
         work,
         mesh=torus,

time: 200 us -> 199 us (level)
  waiting for transfers between devices: 10.7 us -> 6.1 us
  local copies, waits for them, and re-layouts: 8.1 us -> 3.52 us
  Pallas kernels: 17.6 us -> 21.2 us
  blocking collectives: 135 us -> 137 us
    all_to_all x2, waiting for transfers between devices: 6.52 us -> 1.91 us  [exchanged(): return lax.all_to_all(blocks, axis, 0, 0, tiled=True)]
    unnamed x46 -> x36, local copies, waits for them, and re-layouts: 6.53 us -> 1.96 us
    pallas_call x15, Pallas kernels: 17.6 us -> 21.2 us  [call(): pl.pallas_call(kernel, out_shape=outs, in_specs=[pl.BlockSpec(memory_spac...]
    all_to_all x5, blocking collectives: 80.1 us -> 82.6 us  [exchanged(): return lax.all_to_all(blocks, axis, 0, 0, tiled=True)]
  transfers between devices with their start and end apart: 8 -> 8, of which waited for: 5 -> 4; matrix products, arithmetic and copies ran while one was open for 1% -> 1% of each run, Pallas kernels for 6% -> 8%
where the time goes in v2:
time: 199 us; the launch traced here: 195 us
  blocking collectives  137 us (69%)
  starting transfers between devices  26.3 us (13%)
  Pallas kernels  21.2 us (11%)
  waiting for transfers between devices  6.1 us (3%)
  local copies, waits for them, and re-layouts  3.52 us (2%)
    all_to_all x5, blocking collectives, exchanged(): return lax.all_to_all(blocks, axis, 0, 0, tiled=True)  82.6 us
    all_gather x1, blocking collectives, work(): w0 = lax.all_gather(out_weight.T, Z, axis=0, tiled=True)  40.5 us
    pallas_call x15, Pallas kernels, call(): pl.pallas_call(kernel, out_shape=outs, in_specs=[pl.BlockSpec(memory_spac...  21.2 us
    all_gather x1, blocking collectives, work(): own = lax.all_gather(grad_local, 'y', axis=0, tiled=True).reshape(message)  14.2 us
    all_to_all x2, starting transfers between devices, exchanged(): return lax.all_to_all(blocks, axis, 0, 0, tiled=True)  8.42 us
    ppermute x1, starting transfers between devices, work(): wb = lax.ppermute(w1[width:], 'x', ring(NX, -1))  4.57 us
  transfers between devices with their start and end apart: 8, of which 4 were waited for; matrix products, arithmetic and copies ran while one was open for 1% of the time, Pallas kernels for 8%

profile of v2, /device:TPU:24, one launch (start us, length us, event | category | flops | bytes accessed | tf_op | source)
XLA Modules:
  0.0 195.3 jit_solution(250066467325814929)
XLA Ops:
  0.7 40.5 %all_gather.6.w0_ref = bf16[768,512]{1,0:T(8,128)(2,1)S(1)} all-gather(bf16[48,512]{1,0:T(8,128)(2,1)} %bitcast.12), channel_id=1, replica_groups=mesh['x'=4,'zh'=4,'zl'=4,'y'=4,'c'=2] {'zh','zl'}, dimensions={0}, use_global_device_ids=true | all-gather | bytes 835584 | tf_op jit(solution)/shard_map/all_gather | solution.py:338
  41.2 3.4 %collective-permute-start.1 = (bf16[768,512]{1,0:T(8,128)(2,1)S(1)}, bf16[768,512]{1,0:T(8,128)(2,1)S(1)}, u32[]{:S(2)}, u32[]{:S(2)}) collective-permute-start(bf16[768,512]{1,0:T(8,128)(2,1)S(1)} %all_gather.6.w0_ref), channel_id=1, source_target_pairs={{0,128},{128,256},{256,384},{384,0},{1,129},{129,257},{257,385},{3... | collective-permute-start | bytes 2359304 | tf_op jit(solution)/shard_map/ppermute | solution.py:339
  44.6 3.7 %collective-permute-start = (bf16[768,512]{1,0:T(8,128)(2,1)S(1)}, bf16[768,512]{1,0:T(8,128)(2,1)S(1)}, u32[]{:S(2)}, u32[]{:S(2)}) collective-permute-start(bf16[768,512]{1,0:T(8,128)(2,1)S(1)} %all_gather.6.w0_ref), channel_id=1, source_target_pairs={{0,384},{128,0},{256,128},{384,256},{1,385},{129,1},{257,129},{385... | collective-permute-start | bytes 2359304 | tf_op jit(solution)/shard_map/ppermute | solution.py:340
  48.3 2.0 %shard_map.110 = bf16[512,128]{1,0:T(8,128)(2,1)} custom-call(bf16[256,512]{1,0:T(8,128)(2,1)} %k_ref.5, bf16[256,512]{1,0:T(8,128)(2,1)} %v_ref.5), custom_call_target="tpu_custom_call" | custom-call | flops 33554432 | bytes 655360 | tf_op jit(solution)/shard_map/pallas_call | solution.py:32
  50.2 19.7 %all_to_all.35.in_ref = bf16[16,32,128]{2,1,0:T(8,128)(2,1)S(1)} all-to-all(bf16[16,32,128]{2,1,0:T(8,128)(2,1)} %bitcast.11), channel_id=1, replica_groups=mesh['x'=4,'zh'=4,'zl'=4,'y'=4,'c'=2] {'zh','zl'}, dimensions={0} | all-to-all | bytes 262144 | tf_op jit(solution)/shard_map/all_to_all | solution.py:294
  69.9 8.5 %all_to_all.36.offset_ref = f32[4,32,128]{2,1,0:T(8,128)S(1)} all-to-all(f32[4,32,128]{2,1,0:T(8,128)S(1)} %shard_map.111), channel_id=1, replica_groups=mesh['x'=4,'zh'=4,'zl'=4,'y'=4,'c'=2] {'x'}, dimensions={0} | all-to-all | bytes 131072 | tf_op jit(solution)/shard_map/all_to_all | solution.py:294
  79.1 4.2 %all-to-all-start.2 = ((bf16[16,32,128]{2,1,0:T(8,128)(2,1)}), bf16[16,32,128]{2,1,0:T(8,128)(2,1)}, u32[]{:S(2)}, u32[]{:S(2)}) async-start(bf16[16,32,128]{2,1,0:T(8,128)(2,1)} %shard_map.112), calls=%async_computation.2 | async-start | bytes 262144 | tf_op jit(solution)/shard_map/all_to_all | solution.py:294
  83.3 0.8 slice.8
  84.1 2.5 %collective-permute-start.2 = (bf16[384,512]{1,0:T(8,128)(2,1)}, bf16[384,512]{1,0:T(8,128)(2,1)S(1)}, u32[]{:S(2)}, u32[]{:S(2)}) collective-permute-start(bf16[384,512]{1,0:T(8,128)(2,1)} %slice.8), channel_id=1, source_target_pairs={{0,128},{128,256},{256,384},{384,0},{1,129},{129,257},{257,385},{3... | collective-permute-start | bytes 1179656 | tf_op jit(solution)/shard_map/ppermute | solution.py:341
  86.6 0.8 slice.9
  87.3 4.6 %collective-permute-start.3 = (bf16[384,512]{1,0:T(8,128)(2,1)}, bf16[384,512]{1,0:T(8,128)(2,1)S(1)}, u32[]{:S(2)}, u32[]{:S(2)}) collective-permute-start(bf16[384,512]{1,0:T(8,128)(2,1)} %slice.9), channel_id=1, source_target_pairs={{0,384},{128,0},{256,128},{384,256},{1,385},{129,1},{257,129},{385... | collective-permute-start | bytes 1179656 | tf_op jit(solution)/shard_map/ppermute | solution.py:342
  91.9 2.6 %shard_map.109.att_ref = f32[256,512]{1,0:T(8,128)} custom-call(bf16[256,512]{1,0:T(8,128)(2,1)} %q_ref.7, bf16[256,512]{1,0:T(8,128)(2,1)} %k_ref.5, bf16[256,512]{1,0:T(8,128)(2,1)} %v_ref.5), custom_call_target="tpu_custom_call" | custom-call | flops 134217728 | bytes 1310720 | tf_op jit(solution)/shard_map/pallas_call | solution.py:32
  94.5 1.9 all-to-all-done.2
  96.4 1.1 collective-permute-done.3.wb_ref
  97.5 1.2 copy-done.10
  98.7 1.9 shard_map.113
  100.6 1.9 collective-permute-start.4
  102.6 0.7 shard_map.114.keep_ref
  103.3 1.5 collective-permute-done.4.got_ref
  105.0 15.4 %all_to_all.37.got_ref = bf16[4,264,384]{2,1,0:T(8,128)(2,1)S(1)} all-to-all(bf16[4,264,384]{2,1,0:T(8,128)(2,1)S(1)} %shard_map.115), channel_id=1, replica_groups=mesh['x'=4,'zh'=4,'zl'=4,'y'=4,'c'=2] {'y'}, dimensions={0} | all-to-all | bytes 1622016 | tf_op jit(solution)/shard_map/all_to_all | solution.py:294
  120.4 0.9 shard_map.116
  121.3 14.2 %all_gather.7 = bf16[1056,384]{1,0:T(8,128)(2,1)S(1)} all-gather(bf16[264,384]{1,0:T(8,128)(2,1)S(1)} %get-tuple-element.27), channel_id=1, replica_groups=mesh['x'=4,'zh'=4,'zl'=4,'y'=4,'c'=2] {'y'}, dimensions={0}, use_global_device_ids=true | all-gather | bytes 1013760 | tf_op jit(solution)/shard_map/all_gather | solution.py:379
  135.5 1.9 collective-permute-start.5
  138.2 1.5 collective-permute-done.5.other_ref
  139.7 1.4 shard_map.118
  141.9 16.3 %all_to_all.38.in_ref = bf16[16,32,128]{2,1,0:T(8,128)(2,1)S(1)} all-to-all(bf16[16,32,128]{2,1,0:T(8,128)(2,1)S(1)} %bitcast.10), channel_id=1, replica_groups=mesh['x'=4,'zh'=4,'zl'=4,'y'=4,'c'=2] {'x','zl'}, dimensions={0} | all-to-all | bytes 262144 | tf_op jit(solution)/shard_map/all_to_all | solution.py:294
  158.1 22.7 %all_to_all.39.groups_ref = bf16[4,128,128]{2,1,0:T(8,128)(2,1)S(1)} all-to-all(bf16[4,128,128]{2,1,0:T(8,128)(2,1)S(1)} %shard_map.120), channel_id=1, replica_groups=mesh['x'=4,'zh'=4,'zl'=4,'y'=4,'c'=2] {'zh'}, dimensions={0} | all-to-all | bytes 262144 | tf_op jit(solution)/shard_map/all_to_all | solution.py:294
  180.9 0.7 shard_map.121
  181.6 4.3 %all-to-all-start.6 = ((bf16[16,32,128]{2,1,0:T(8,128)(2,1)}), bf16[16,32,128]{2,1,0:T(8,128)(2,1)S(1)}, u32[]{:S(2)}, u32[]{:S(2)}) async-start(bf16[16,32,128]{2,1,0:T(8,128)(2,1)} %shard_map.121), calls=%async_computation.6 | async-start | bytes 262144 | tf_op jit(solution)/shard_map/all_to_all | solution.py:294
  185.9 3.7 %shard_map.119 = (bf16[256,512]{1,0:T(8,128)(2,1)}, f32[256,512]{1,0:T(8,128)}, f32[256,512]{1,0:T(8,128)}) custom-call(bf16[256,512]{1,0:T(8,128)(2,1)} %q_ref.7, bf16[256,512]{1,0:T(8,128)(2,1)} %k_ref.5, bf16[256,512]{1,0:T(8,128)(2,1)} %v_ref.5, bf16[256,512]{1,0:T(8,128)(2,1)} %copy-done.16, bf16[512,128]{1,0:T(8,128)(2,1)} %bitcast.1.state_ref), custom_call_target="tpu_custom_call" | custom-call | flops 369098752 | bytes 2490368 | tf_op jit(solution)/shard_map/pallas_call | solution.py:32
  189.6 4.7 %shard_map.123 = bf16[1,512,3072]{2,1,0:T(8,128)(2,1)} custom-call(bf16[4,264,384]{2,1,0:T(8,128)(2,1)} %bitcast.8, bf16[4,264,384]{2,1,0:T(8,128)(2,1)} %copy-done.5, f32[256,512]{1,0:T(8,128)} %copy-done.9, bf16[1,512]{1,0:T(2,128)(2,1)} %copy-done.14, f32[8,256]{1,0:T(8,128)} %copy-done.15), custom_call_target="tpu_custom_call" | custom-call | flops 805306368 | bytes 5301248 | tf_op jit(solution)/shard_map/pallas_call | solution.py:32
  194.3 1.1 shard_map.122
  (45 shorter events, 2.4 us)
Async XLA Ops:
  0.6 91.3 %copy-start.17 = (bf16[512]{0:T(512)(128)(2,1)S(1)}, bf16[512]{0:T(512)(128)(2,1)}, u32[]{:S(2)}) copy-start(bf16[512]{0:T(512)(128)(2,1)} %param.9) | copy-start | bytes 3076
  0.6 96.9 %copy-start.6 = (bf16[256,512]{1,0:T(8,128)(2,1)S(1)}, bf16[256,512]{1,0:T(8,128)(2,1)}, u32[]{:S(2)}) copy-start(bf16[256,512]{1,0:T(8,128)(2,1)} %q_ref.7) | copy-start | bytes 786436
  41.2 42.1 %collective-permute-start.1 = (bf16[768,512]{1,0:T(8,128)(2,1)S(1)}, bf16[768,512]{1,0:T(8,128)(2,1)S(1)}, u32[]{:S(2)}, u32[]{:S(2)}) collective-permute-start(bf16[768,512]{1,0:T(8,128)(2,1)S(1)} %all_gather.6.w0_ref), channel_id=1, source_target_pairs={{0,128},{128,256},{256,384},{384,0},{1,129},{129,257},{257,385},{3... | collective-permute-start | bytes 2359304 | tf_op jit(solution)/shard_map/ppermute | solution.py:339
  44.6 42.0 %collective-permute-start = (bf16[768,512]{1,0:T(8,128)(2,1)S(1)}, bf16[768,512]{1,0:T(8,128)(2,1)S(1)}, u32[]{:S(2)}, u32[]{:S(2)}) collective-permute-start(bf16[768,512]{1,0:T(8,128)(2,1)S(1)} %all_gather.6.w0_ref), channel_id=1, source_target_pairs={{0,384},{128,0},{256,128},{384,256},{1,385},{129,1},{257,129},{385... | collective-permute-start | bytes 2359304 | tf_op jit(solution)/shard_map/ppermute | solution.py:340
  79.1 17.3 %all-to-all-start.2 = ((bf16[16,32,128]{2,1,0:T(8,128)(2,1)}), bf16[16,32,128]{2,1,0:T(8,128)(2,1)}, u32[]{:S(2)}, u32[]{:S(2)}) async-start(bf16[16,32,128]{2,1,0:T(8,128)(2,1)} %shard_map.112), calls=%async_computation.2 | async-start | bytes 262144 | tf_op jit(solution)/shard_map/all_to_all | solution.py:294
  84.1 12.3 %collective-permute-start.2 = (bf16[384,512]{1,0:T(8,128)(2,1)}, bf16[384,512]{1,0:T(8,128)(2,1)S(1)}, u32[]{:S(2)}, u32[]{:S(2)}) collective-permute-start(bf16[384,512]{1,0:T(8,128)(2,1)} %slice.8), channel_id=1, source_target_pairs={{0,128},{128,256},{256,384},{384,0},{1,129},{129,257},{257,385},{3... | collective-permute-start | bytes 1179656 | tf_op jit(solution)/shard_map/ppermute | solution.py:341
  87.3 10.2 %collective-permute-start.3 = (bf16[384,512]{1,0:T(8,128)(2,1)}, bf16[384,512]{1,0:T(8,128)(2,1)S(1)}, u32[]{:S(2)}, u32[]{:S(2)}) collective-permute-start(bf16[384,512]{1,0:T(8,128)(2,1)} %slice.9), channel_id=1, source_target_pairs={{0,384},{128,0},{256,128},{384,256},{1,385},{129,1},{257,129},{385... | collective-permute-start | bytes 1179656 | tf_op jit(solution)/shard_map/ppermute | solution.py:342
  91.9 47.8 %copy-start.14 = (bf16[1,512]{1,0:T(2,128)(2,1)}, bf16[1,512]{1,0:T(2,128)(2,1)S(1)}, u32[]{:S(2)}) copy-start(bf16[1,512]{1,0:T(2,128)(2,1)S(1)} %reshape.32.gain_ref) | copy-start | bytes 3076
  96.4 6.9 %copy-start.1 = (bf16[384,512]{1,0:T(8,128)(2,1)}, bf16[384,512]{1,0:T(8,128)(2,1)S(1)}, u32[]{:S(2)}) copy-start(bf16[384,512]{1,0:T(8,128)(2,1)S(1)} %collective-permute-done.2.wa_ref) | copy-start | bytes 1179652
  97.5 5.8 %copy-start.3 = (bf16[384,512]{1,0:T(8,128)(2,1)}, bf16[384,512]{1,0:T(8,128)(2,1)S(1)}, u32[]{:S(2)}) copy-start(bf16[384,512]{1,0:T(8,128)(2,1)S(1)} %collective-permute-done.3.wb_ref) | copy-start | bytes 1179652
  97.5 1.2 copy-start.10
  100.6 39.1 %copy-start.9 = (f32[256,512]{1,0:T(8,128)}, f32[256,512]{1,0:T(8,128)S(1)}, u32[]{:S(2)}) copy-start(f32[256,512]{1,0:T(8,128)S(1)} %get-tuple-element.30.mixed_ref) | copy-start | bytes 1572868
  100.6 4.2 %collective-permute-start.4 = (bf16[4,264,384]{2,1,0:T(8,128)(2,1)S(1)}, bf16[4,264,384]{2,1,0:T(8,128)(2,1)S(1)}, u32[]{:S(2)}, u32[]{:S(2)}) collective-permute-start(bf16[4,264,384]{2,1,0:T(8,128)(2,1)S(1)} %get-tuple-element.24), channel_id=1, source_target_pairs={{0,1},{1,0},{2,3},{3,2},{4,5},{5,4},{6,7},{7,6},{8,9},{9,8},{10,11... | collective-permute-start | bytes 2433032 | tf_op jit(solution)/shard_map/ppermute | solution.py:367
  103.3 17.1 %copy-start.13 = (bf16[256,384]{1,0:T(8,128)(2,1)S(1)}, bf16[256,384]{1,0:T(8,128)(2,1)}, u32[]{:S(2)}) copy-start(bf16[256,384]{1,0:T(8,128)(2,1)} %target_ref.1) | copy-start | bytes 589828
  104.9 32.6 %copy-start.2 = (bf16[384,512]{1,0:T(8,128)(2,1)S(1)}, bf16[384,512]{1,0:T(8,128)(2,1)}, u32[]{:S(2)}) copy-start(bf16[384,512]{1,0:T(8,128)(2,1)} %copy-done.1) | copy-start | bytes 1179652
  104.9 32.6 %copy-start.4 = (bf16[384,512]{1,0:T(8,128)(2,1)S(1)}, bf16[384,512]{1,0:T(8,128)(2,1)}, u32[]{:S(2)}) copy-start(bf16[384,512]{1,0:T(8,128)(2,1)} %copy-done.3) | copy-start | bytes 1179652
  121.3 19.8 %copy-start.15 = (f32[8,256]{1,0:T(8,128)}, f32[8,256]{1,0:T(8,128)S(1)}, u32[]{:S(2)}) copy-start(f32[8,256]{1,0:T(8,128)S(1)} %get-tuple-element.31.inverse_ref) | copy-start | bytes 24580
  135.5 5.6 %copy-start = (bf16[1056,384]{1,0:T(8,128)(2,1)}, bf16[1056,384]{1,0:T(8,128)(2,1)S(1)}, u32[]{:S(2)}) copy-start(bf16[1056,384]{1,0:T(8,128)(2,1)S(1)} %all_gather.7) | copy-start | bytes 2433028
  135.5 4.2 %collective-permute-start.5 = (bf16[4,264,384]{2,1,0:T(8,128)(2,1)S(1)}, bf16[4,264,384]{2,1,0:T(8,128)(2,1)S(1)}, u32[]{:S(2)}, u32[]{:S(2)}) collective-permute-start(bf16[4,264,384]{2,1,0:T(8,128)(2,1)S(1)} %bitcast.6), channel_id=1, source_target_pairs={{0,1},{1,0},{2,3},{3,2},{4,5},{5,4},{6,7},{7,6},{8,9},{9,8},{10,11... | collective-permute-start | bytes 2433032 | tf_op jit(solution)/shard_map/ppermute | solution.py:380
  139.7 2.1 %copy-start.5 = (bf16[4,264,384]{2,1,0:T(8,128)(2,1)}, bf16[4,264,384]{2,1,0:T(8,128)(2,1)S(1)}, u32[]{:S(2)}) copy-start(bf16[4,264,384]{2,1,0:T(8,128)(2,1)S(1)} %collective-permute-done.5.other_ref) | copy-start | bytes 2433028
  141.2 0.7 copy-start.16
  181.6 12.7 %all-to-all-start.6 = ((bf16[16,32,128]{2,1,0:T(8,128)(2,1)}), bf16[16,32,128]{2,1,0:T(8,128)(2,1)S(1)}, u32[]{:S(2)}, u32[]{:S(2)}) async-start(bf16[16,32,128]{2,1,0:T(8,128)(2,1)} %shard_map.121), calls=%async_computation.6 | async-start | bytes 262144 | tf_op jit(solution)/shard_map/all_to_all | solution.py:294
  185.9 8.4 %copy-start.7 = (bf16[256,512]{1,0:T(8,128)(2,1)S(1)}, bf16[256,512]{1,0:T(8,128)(2,1)}, u32[]{:S(2)}) copy-start(bf16[256,512]{1,0:T(8,128)(2,1)} %k_ref.5) | copy-start | bytes 786436
  185.9 8.4 %copy-start.8 = (bf16[256,512]{1,0:T(8,128)(2,1)S(1)}, bf16[256,512]{1,0:T(8,128)(2,1)}, u32[]{:S(2)}) copy-start(bf16[256,512]{1,0:T(8,128)(2,1)} %v_ref.5) | copy-start | bytes 786436
  189.6 4.7 %copy-start.11 = (f32[256,512]{1,0:T(8,128)S(1)}, f32[256,512]{1,0:T(8,128)}, u32[]{:S(2)}) copy-start(f32[256,512]{1,0:T(8,128)} %get-tuple-element.34.key_part_ref) | copy-start | bytes 1572868
  189.6 4.7 %copy-start.12 = (f32[256,512]{1,0:T(8,128)S(1)}, f32[256,512]{1,0:T(8,128)}, u32[]{:S(2)}) copy-start(f32[256,512]{1,0:T(8,128)} %get-tuple-element.35.value_part_ref) | copy-start | bytes 1572868
